TPU v7x, 256 devices: a 2x2x32 block of a 4x8x32 slice. The times are simulated.
256 devices in a mesh: group: 4 (over y, x), space: 64 (over z, core).
Axes of the slice: x: 2, y: 2, z: 32, core: 2. Of those that a mesh axis runs over, the one named last changes fastest.
The devices are a block of a 4x8x32 slice.
Arguments:
- images: float32 [8, 128, 128, 128], P('group', 'space'), parts along dimension 0, may hold values from -2.7 to 2.7
- weights: float32 [8, 2], P('group'), parts along dimension 0, may hold values from 0 to 1
Outputs:
- relaxed: float32 [8, 128, 128, 128], P('group', 'space'), parts along dimension 0
- spacing: float32 [8, 1], P('group'), parts along dimension 0
There are 4 independent parts, one for each index of `group`. A program takes and returns all parts, laid end to end along the dimension named above; each array names one. Nothing has to cross between parts.
All inputs are finite; a program needn't handle non-finite values.
Results may differ from a plain program's by a relative error of at most 0.0002.
Values sent between devices are 32-bit elements; how exact they have to be, the bound alone decides.
A program may use at most 64 MiB of HBM per device.

v0:
```python
import math

import jax
import jax.numpy as jnp
from jax import lax
from jax.sharding import PartitionSpec as P

ITERS = 2


highest = lax.Precision.HIGHEST
time_step = 0.1
gradient_weight = 1.0


def sent_to_all(shard, axis):
    copies = jnp.broadcast_to(shard, (lax.axis_size(axis), *shard.shape))
    return lax.all_to_all(copies, axis, split_axis=0, concat_axis=0, tiled=True)


def taken_together(shard, axis):
    return sent_to_all(shard, axis).sum(axis=0)


def paired_order(length, position):
    halves = position // 2
    parity = position % 2
    return jnp.where(parity == 0, halves, jnp.where(halves == 0, length // 2, length - halves))


def dft_tables(length, outputs, inputs, factor):
    product = outputs[:, None] * inputs[None, :] % length
    angles = product.astype(jnp.float32) * (2.0 * math.pi / length)
    return (jnp.cos(angles) * factor, jnp.sin(angles) * factor)


def wave_squares(length, indices):
    signed = jnp.where(indices <= length // 2, indices, indices - length)
    number = signed.astype(jnp.float32) * (2.0 * math.pi / length)
    return number * number


def along_first(values, matrix):
    return jnp.einsum("...xyz,kx->...kyz", values, matrix, precision=highest)


def along_second(values, matrix):
    return jnp.einsum("...xyz,ky->...xkz", values, matrix, precision=highest)


def along_third(values, matrix):
    return jnp.einsum("...xyz,kz->...xyk", values, matrix, precision=highest)


def complex_pass(real_part, imag_part, tables, along, signum):
    cosine, sine_table = tables
    return (
        along(real_part, cosine) + signum * along(imag_part, sine_table),
        along(imag_part, cosine) - signum * along(real_part, sine_table),
    )


def reflect(values, axis_number):
    length = values.shape[axis_number]
    leading = lax.slice_in_dim(values, 0, 1, axis=axis_number)
    remainder = jnp.flip(lax.slice_in_dim(values, 1, length, axis=axis_number), axis_number)
    return jnp.concatenate([leading, remainder], axis_number)


def mirror(values, self_paired):
    dimensions = values.ndim
    flipped = reflect(reflect(values, dimensions - 3), dimensions - 1)
    extent = flipped.shape
    grouped = extent[: dimensions - 2] + (extent[dimensions - 2] // 2, 2) + extent[dimensions - 1 :]
    swapped = jnp.flip(flipped.reshape(grouped), dimensions - 1).reshape(extent)
    return jnp.where(self_paired, flipped, swapped)


def local(images, weights):
    image_count, first_local, second_length, third_length = images.shape
    space_size = lax.axis_size("space")
    position = lax.axis_index("space")
    first_length = first_local * space_size
    second_local = second_length // space_size
    first_index = jnp.arange(first_length, dtype=jnp.int32)
    second_index = jnp.arange(second_length, dtype=jnp.int32)
    third_index = jnp.arange(third_length, dtype=jnp.int32)
    second_order = paired_order(second_length, second_index)
    first_forward = dft_tables(first_length, first_index, first_index, 1.0)
    first_inverse = dft_tables(first_length, first_index, first_index, 1.0 / first_length)
    second_forward = dft_tables(second_length, second_order, second_index, 1.0)
    second_inverse = dft_tables(second_length, second_index, second_order, 1.0 / second_length)
    third_forward = dft_tables(third_length, third_index, third_index, 1.0)
    third_inverse = dft_tables(third_length, third_index, third_index, 1.0 / third_length)
    local_rows = position * second_local + jnp.arange(second_local, dtype=jnp.int32)
    self_paired = (local_rows < 2)[:, None]
    squares = (
        wave_squares(first_length, first_index)[:, None, None]
        + wave_squares(second_length, paired_order(second_length, local_rows))[None, :, None]
        + wave_squares(third_length, third_index)[None, None, :]
    )
    damping = 1.0 / (1.0 + time_step * gradient_weight * squares * squares)
    coupling = time_step * squares * damping
    cell_count = first_length * second_length * third_length
    concentration = images
    partials = []
    for iteration in range(ITERS):
        potential = concentration * concentration * concentration - concentration
        grouped = (image_count // 2, 2, first_local, second_length, third_length)
        real_part, imag_part = complex_pass(
            concentration.reshape(grouped),
            potential.reshape(grouped),
            third_forward,
            along_third,
            1.0,
        )
        real_part, imag_part = complex_pass(real_part, imag_part, second_forward, along_second, 1.0)
        spectra = jnp.stack([real_part, imag_part], 2)
        relax_incoming = lax.all_to_all(spectra, "space", split_axis=4, concat_axis=3, tiled=True)
        relax_real_part, relax_imag_part = complex_pass(
            relax_incoming[:, :, 0], relax_incoming[:, :, 1], first_forward, along_first, 1.0
        )
        mirror_real = mirror(relax_real_part, self_paired)
        mirror_imag = mirror(relax_imag_part, self_paired)
        relax_new_real = (
            0.5 * (relax_real_part + mirror_real) * damping
            - 0.5 * (relax_imag_part + mirror_imag) * coupling
        )
        relax_new_imag = (
            0.5 * (relax_imag_part - mirror_imag) * damping
            - 0.5 * (mirror_real - relax_real_part) * coupling
        )
        packed_real = relax_new_real[:, 0] - relax_new_imag[:, 1]
        packed_imag = relax_new_imag[:, 0] + relax_new_real[:, 1]
        new_real = packed_real
        new_imag = packed_imag
        new_real, new_imag = complex_pass(new_real, new_imag, first_inverse, along_first, -1.0)
        new_real, new_imag = complex_pass(new_real, new_imag, third_inverse, along_third, -1.0)
        partial_value = jnp.stack([new_real, new_imag], 1)
        incoming = lax.all_to_all(partial_value, "space", split_axis=2, concat_axis=3, tiled=True)
        cosine, sine_table = second_inverse
        finish_real_part = along_second(incoming[:, 0], cosine) - along_second(
            incoming[:, 1], sine_table
        )
        finish_imag_part = along_second(incoming[:, 1], cosine) + along_second(
            incoming[:, 0], sine_table
        )
        paired = jnp.stack([finish_real_part, finish_imag_part], 1)
        concentration = paired.reshape(images.shape)
        difference = concentration[1:] - concentration[:-1]
        partial_sum = jnp.sum(difference * difference, axis=(1, 2, 3))
        partials.append(partial_sum)
        concentration = jnp.einsum("ij,jxyz->ixyz", weights, concentration, precision=highest)
    spacing = taken_together(jnp.stack(partials), "space") / cell_count
    return (concentration, spacing)


def solution(mesh):
    placed = (P("group", "space", None, None), P("group", None))
    return jax.shard_map(
        local,
        mesh=mesh,
        in_specs=placed,
        out_specs=(P("group", "space", None, None), P("group", None)),
        check_vma=False,
    )
```

profile of v0, /device:TPU:37, one launch (start us, length us, event | category | flops | bytes accessed | tf_op | source)
XLA Modules:
  0.0 335.0 jit_solution(7606342751130329577)
XLA Ops:
  0.7 1.7 convolution_bitcast_fusion.1
  3.0 0.7 convolution_add_fusion.5
  4.3 0.7 fusion.80
  4.9 0.7 fusion.78
  5.6 0.7 fusion.7
  6.3 0.7 fusion.6
  7.1 1.2 copy.42
  8.3 34.9 %all-to-all-start = ((f32[1,2,2,2,128,128]{5,3,1,2,0,4:T(2,128)}), f32[1,2,2,2,128,128]{5,3,1,2,0,4:T(2,128)S(1)}, u32[]{:S(2)}, u32[]{:S(2)}) async-start(f32[1,2,2,2,128,128]{5,3,1,2,0,4:T(2,128)} %copy.42), calls=%async_computation | async-start | bytes 1048576 | tf_op jit(solution)/shard_map/all_to_all | solution.py:119
  43.4 63.3 %all-to-all-done = f32[1,2,2,2,128,128]{5,3,1,2,0,4:T(2,128)S(1)} async-done(((f32[1,2,2,2,128,128]{5,3,1,2,0,4:T(2,128)}), f32[1,2,2,2,128,128]{5,3,1,2,0,4:T(2,128)S(1)}, u32[]{:S(2)}, u32[]{:S(2)}) %all-to-all-start) | async-done | bytes 524320 | tf_op jit(solution)/shard_map/all_to_all | solution.py:119
  106.9 0.6 fusion.19
  107.6 0.6 fusion.4
  108.6 0.6 fusion.18
  109.3 0.6 fusion.5
  115.9 48.0 %all_to_all.77 = f32[1,2,128,2,128]{4,3,1,0,2:T(2,128)S(1)} all-to-all(f32[1,2,128,2,128]{4,3,1,0,2:T(2,128)S(1)} %copy.44), channel_id=1, replica_groups=mesh['group'=4,'space'=64] {'space'}, dimensions={2} | all-to-all | bytes 524288 | tf_op jit(solution)/shard_map/all_to_all | solution.py:140
  165.6 1.1 fusion.35
  166.7 1.1 fusion.16
  169.7 0.7 fusion.76
  171.0 0.7 fusion.74
  171.7 0.7 fusion.3
  172.4 0.7 fusion.2
  173.6 68.4 %all_to_all.78 = f32[1,2,2,2,128,128]{5,3,1,2,0,4:T(2,128)S(1)} all-to-all(f32[1,2,2,2,128,128]{5,3,1,2,0,4:T(2,128)S(1)} %copy.48), channel_id=1, replica_groups=mesh['group'=4,'space'=64] {'space'}, dimensions={4} | all-to-all | bytes 1048576 | tf_op jit(solution)/shard_map/all_to_all | solution.py:119
  242.2 0.6 fusion.21
  242.9 0.6 fusion
  243.9 0.6 fusion.20
  244.6 0.6 fusion.1
  251.3 49.6 %all_to_all.79 = f32[1,2,128,2,128]{4,3,1,0,2:T(2,128)S(1)} all-to-all(f32[1,2,128,2,128]{4,3,1,0,2:T(2,128)S(1)} %copy.50), channel_id=1, replica_groups=mesh['group'=4,'space'=64] {'space'}, dimensions={2} | all-to-all | bytes 524288 | tf_op jit(solution)/shard_map/all_to_all | solution.py:140
  302.6 1.1 fusion.33
  303.7 1.4 maximum_bitcast_fusion.2
  305.7 5.5 %all-to-all-start.4 = ((f32[64,2,1]{1,2,0:T(1,128)}), f32[64,2,1]{1,2,0:T(1,128)S(1)}, u32[]{:S(2)}, u32[]{:S(2)}) async-start(f32[64,2,1]{1,2,0:T(1,128)} %broadcast_in_dim.30), calls=%async_computation.4 | async-start | bytes 65536 | tf_op jit(solution)/shard_map/all_to_all | solution.py:18
  311.3 1.1 convolution_bitcast_fusion.2
  312.3 0.7 copy.53
  313.1 20.9 %all-to-all-done.4 = f32[64,2,1]{1,2,0:T(1,128)S(1)} async-done(((f32[64,2,1]{1,2,0:T(1,128)}), f32[64,2,1]{1,2,0:T(1,128)S(1)}, u32[]{:S(2)}, u32[]{:S(2)}) %all-to-all-start.4) | async-done | bytes 544 | tf_op jit(solution)/shard_map/all_to_all | solution.py:18
  (83 shorter events, 21.9 us)
Async XLA Ops:
  0.6 166.1 %copy-start = (f32[2,2]{1,0:T(2,128)S(1)}, f32[2,2]{1,0:T(2,128)}, u32[]{:S(2)}) copy-start(f32[2,2]{1,0:T(2,128)} %param.3) | copy-start | bytes 52
  0.7 1.7 copy-start.1
  8.3 98.5 %all-to-all-start = ((f32[1,2,2,2,128,128]{5,3,1,2,0,4:T(2,128)}), f32[1,2,2,2,128,128]{5,3,1,2,0,4:T(2,128)S(1)}, u32[]{:S(2)}, u32[]{:S(2)}) async-start(f32[1,2,2,2,128,128]{5,3,1,2,0,4:T(2,128)} %copy.42), calls=%async_computation | async-start | bytes 1048576 | tf_op jit(solution)/shard_map/all_to_all | solution.py:119
  305.7 28.3 %all-to-all-start.4 = ((f32[64,2,1]{1,2,0:T(1,128)}), f32[64,2,1]{1,2,0:T(1,128)S(1)}, u32[]{:S(2)}, u32[]{:S(2)}) async-start(f32[64,2,1]{1,2,0:T(1,128)} %broadcast_in_dim.30), calls=%async_computation.4 | async-start | bytes 65536 | tf_op jit(solution)/shard_map/all_to_all | solution.py:18
where the time goes:
time: 341 us; the launch traced here: 335 us
  blocking collectives  166 us (49%)
  waiting for transfers between devices  84.2 us (25%)
  starting transfers between devices  40.4 us (12%)
  matrix products  32.4 us (10%)
  local copies, waits for them, and re-layouts  6.27 us (2%)
  other arithmetic  3.91 us (1%)
    all_to_all x2, blocking collectives, local(): lax.all_to_all(partial_value, 'space', split_axis=2, concat_axis=3, tiled...  97.6 us
    all_to_all x1, blocking collectives, local(): lax.all_to_all(spectra, 'space', split_axis=4, concat_axis=3, tiled=True)  68.4 us
    all_to_all x1, waiting for transfers between devices, local(): lax.all_to_all(spectra, 'space', split_axis=4, concat_axis=3, tiled=True)  63.3 us
    all_to_all x1, starting transfers between devices, local(): lax.all_to_all(spectra, 'space', split_axis=4, concat_axis=3, tiled=True)  34.9 us
    all_to_all x1, waiting for transfers between devices, sent_to_all(): return lax.all_to_all(copies, axis, split_axis=0, concat_axis=0, tiled=True)  20.9 us
    dot_general x16, matrix products, along_second(): return jnp.einsum('...xyz,ky->...xkz', values, matrix, precision=highest)  10.8 us
    dot_general x16, matrix products, along_third(): return jnp.einsum('...xyz,kz->...xyk', values, matrix, precision=highest)  10.1 us
    dot_general x16, matrix products, along_first(): return jnp.einsum('...xyz,kx->...kyz', values, matrix, precision=highest)  9.28 us
  transfers between devices with their start and end apart: 2, of which 2 were waited for; matrix products, arithmetic and copies ran while one was open for 1% of the time, Pallas kernels for 0%

commit v1 on v0

v1 whole, which is shorter than its diff:
```python
import functools
import math

import jax
import jax.numpy as jnp
import numpy as np
from jax import lax
from jax.experimental import pallas as pl
from jax.experimental.pallas import tpu as pltpu
from jax.sharding import PartitionSpec as P

ITERS = 2
CORES = 2
SUBLANES = 8
time_step = 0.1
gradient_weight = 1.0


def frequencies(length):
    half = length // 2
    return np.concatenate([np.arange(half), [half], np.arange(1, half)])


def real_basis(length):
    half = length // 2
    cells = np.arange(length)
    product = np.outer(frequencies(length), cells) % length
    angles = product * (2.0 * math.pi / length)
    rows = np.where(np.arange(length)[:, None] <= half, np.cos(angles), np.sin(angles)) * math.sqrt(2.0 / length)
    rows[[0, half]] *= math.sqrt(0.5)
    return rows


def wave_squares(length):
    return (frequencies(length) * (2.0 * math.pi / length)) ** 2


def split(value):
    high = value.astype(jnp.bfloat16)
    return high, (value - high.astype(jnp.float32)).astype(jnp.bfloat16)


def product(left, right):
    dot = functools.partial(jnp.dot, preferred_element_type=jnp.float32)
    return dot(left[0], right[0]) + (dot(left[0], right[1]) + dot(left[1], right[0]))


def kernel(
    shape, axis_size,
    images_ref, weights_ref, qy_ref, qyt_ref, qz_ref, qzt_ref, qx_ref, qxt_ref, sqx_ref, sqz_ref,
    out_ref, spacing_ref,
    first_send, first_recv, back_send, back_recv, next_send, next_recv, last_send, last_recv,
    part_send, part_recv, field_spectrum, send_sem, recv_sem,
):
    image_count, planes, second_length, third_length = shape
    half = second_length // 2
    chips = axis_size // CORES
    me = lax.axis_index("space")
    group = lax.axis_index("group")
    my_chip, my_core = me // CORES, me % CORES

    def partner(offset, core):
        return lax.rem(my_chip + offset + chips, chips) * CORES + core

    barrier = pltpu.get_barrier_semaphore()

    def greet(step, carry):
        pl.semaphore_signal(
            barrier, inc=1, device_id=(group, lax.rem(me + step, axis_size)), device_id_type=pl.DeviceIdType.MESH
        )
        return carry

    lax.fori_loop(1, axis_size, greet, 0)

    def exchange(send, recv, phase):
        def copy_to(target):
            pltpu.make_async_remote_copy(
                src_ref=send.at[target],
                dst_ref=recv.at[me],
                send_sem=send_sem.at[phase],
                recv_sem=recv_sem.at[phase],
                device_id=(group, target),
                device_id_type=pl.DeviceIdType.MESH,
            ).start()

        copy_to(partner(chips // 2, my_core))
        copy_to(partner(chips // 2, 1 - my_core))

        def step(i, carry):
            distance = chips // 2 - 1 - i
            copy_to(partner(distance, my_core))
            copy_to(partner(-distance, my_core))
            copy_to(partner(distance, 1 - my_core))
            copy_to(partner(-distance, 1 - my_core))
            return carry

        lax.fori_loop(0, chips // 2 - 1, step, 0)
        copy_to(partner(0, 1 - my_core))

    def finish(send, recv, phase):
        others = pl.ds(0, axis_size - 1)
        pltpu.make_async_copy(recv.at[others], recv.at[others], recv_sem.at[phase]).wait()
        pltpu.make_async_copy(send.at[others], send.at[others], send_sem.at[phase]).wait()

    def rows_of(field, image, plane, parity):
        return ((field * image_count + image) * planes + plane) * 2 + parity

    def spread(send, row, value):
        send[:, row // SUBLANES, row % SUBLANES, :] = value

    def gathered(recv, row):
        return recv[:, row // SUBLANES, row % SUBLANES, :]

    qy, qyt = (qy_ref[0], qy_ref[1]), (qyt_ref[0], qyt_ref[1])
    qz, qzt = (qz_ref[0], qz_ref[1]), (qzt_ref[0], qzt_ref[1])
    qx, qxt = (qx_ref[0], qx_ref[1]), (qxt_ref[0], qxt_ref[1])

    def forward_slab(value, send, field, image, plane):
        along_third = product(split(value), qzt)
        spectrum = product(qy, split(along_third))
        for parity in range(2):
            spread(send, rows_of(field, image, plane, parity), spectrum[parity * half : (parity + 1) * half])

    def backward_slab(recv, image, plane):
        spectrum = jnp.concatenate([gathered(recv, rows_of(0, image, plane, parity)) for parity in range(2)], 0)
        along_second = product(qyt, split(spectrum))
        return product(split(along_second), qz)

    def forward_pencils(recv, field):
        columns = [
            jnp.concatenate([gathered(recv, rows_of(field, image, plane, parity)) for plane in range(planes)], 0)
            for image in range(image_count)
            for parity in range(2)
        ]
        return product(qx, split(jnp.concatenate(columns, 1)))

    def backward_pencils(spectrum, send):
        columns = product(qxt, split(spectrum))
        for image in range(image_count):
            for plane in range(planes):
                for parity in range(2):
                    start = (image * 2 + parity) * third_length
                    spread(
                        send, rows_of(0, image, plane, parity),
                        columns[plane * axis_size : (plane + 1) * axis_size, start : start + third_length],
                    )

    def potential(value):
        return value * value * value - value

    for image in range(image_count):
        for plane in range(planes):
            value = images_ref[image, plane]
            forward_slab(value, first_send, 0, image, plane)
            forward_slab(potential(value), first_send, 1, image, plane)
    first_recv[me] = first_send[me]
    pl.semaphore_wait(barrier, axis_size - 1)
    exchange(first_send, first_recv, 0)

    number = 2.0 * math.pi / second_length
    cosine_number = me.astype(jnp.float32) * number
    other_number = jnp.where(me == 0, jnp.float32(half), me.astype(jnp.float32)) * number
    squares = jnp.concatenate(
        [sqx_ref[...] + sqz_ref[...] + square for square in (cosine_number * cosine_number, other_number * other_number)], 1
    )
    damping = 1.0 / (1.0 + time_step * gradient_weight * squares * squares)
    coupling = time_step * squares * damping
    width = 2 * third_length

    def image_of(value, image):
        return value[:, image * width : (image + 1) * width]

    def mixed(values):
        new = []
        for i in range(image_count):
            total = weights_ref[i, 0] * values[0]
            for j in range(1, image_count):
                total = total + weights_ref[i, j] * values[j]
            new.append(total)
        return new

    def new_spectra(field_parts, potential_parts):
        return [damping * field_parts[i] - coupling * image_of(potential_parts, i) for i in range(image_count)]

    lane = lax.broadcasted_iota(jnp.int32, (1, third_length), 1)

    def spacing_parts(values, row, iteration):
        for j in range(image_count - 1):
            difference = values[j + 1] - values[j]
            row = jnp.where(lane == iteration * (image_count - 1) + j, jnp.sum(difference * difference), row)
        return row

    finish(first_send, first_recv, 0)
    field_parts = forward_pencils(first_recv, 0)
    spectra = new_spectra([image_of(field_parts, i) for i in range(image_count)], forward_pencils(first_recv, 1))
    parts = spacing_parts(spectra, jnp.zeros((1, third_length), jnp.float32), 0)
    spectra = mixed(spectra)
    backward_pencils(jnp.concatenate(spectra, 1), back_send)
    back_recv[me] = back_send[me]
    exchange(back_send, back_recv, 1)
    field_spectrum[...] = jnp.concatenate(spectra, 1)

    finish(back_send, back_recv, 1)
    for image in range(image_count):
        for plane in range(planes):
            forward_slab(potential(backward_slab(back_recv, image, plane)), next_send, 0, image, plane)
    next_recv[me] = next_send[me]
    exchange(next_send, next_recv, 2)

    finish(next_send, next_recv, 2)
    spectra = new_spectra([image_of(field_spectrum, i) for i in range(image_count)], forward_pencils(next_recv, 0))
    part_send[0] = spacing_parts(spectra, parts, 1)
    backward_pencils(jnp.concatenate(mixed(spectra), 1), last_send)
    last_recv[me] = last_send[me]

    def part_to(step, carry):
        target = lax.rem(me + step, axis_size)
        pltpu.make_async_remote_copy(
            src_ref=part_send.at[0],
            dst_ref=part_recv.at[me],
            send_sem=send_sem.at[4],
            recv_sem=recv_sem.at[4],
            device_id=(group, target),
            device_id_type=pl.DeviceIdType.MESH,
        ).start()
        return carry

    lax.fori_loop(1, axis_size, part_to, 0)
    part_recv[me] = part_send[0]
    exchange(last_send, last_recv, 3)

    finish(last_send, last_recv, 3)
    for image in range(image_count):
        for plane in range(planes):
            out_ref[image, plane] = backward_slab(last_recv, image, plane)
    others = pl.ds(0, axis_size - 1)
    pltpu.make_async_copy(part_recv.at[others], part_recv.at[others], recv_sem.at[4]).wait()
    pltpu.make_async_copy(part_recv.at[others], part_recv.at[others], send_sem.at[4]).wait()
    cell_count = planes * axis_size * second_length * third_length
    totals = jnp.sum(part_recv[...], axis=0) / cell_count
    for iteration in range(ITERS):
        first = iteration * (image_count - 1)
        spacing_ref[iteration : iteration + 1, :] = totals[:, first : first + image_count - 1]


def two_parts(matrix):
    matrix = matrix.astype(np.float32)
    high = matrix.astype(jnp.bfloat16)
    low = (matrix - high.astype(np.float32)).astype(jnp.bfloat16)
    return np.stack([high, low])


def local(axis_size, images, weights):
    image_count, planes, second_length, third_length = images.shape
    first_length = planes * axis_size
    assert second_length == 2 * axis_size and axis_size % (2 * CORES) == 0
    basis_x = real_basis(first_length)
    order = np.arange(first_length).reshape(axis_size, planes).T.reshape(-1)
    basis_x = basis_x[:, order]
    basis_y, basis_z = real_basis(second_length), real_basis(third_length)
    tables = [two_parts(m) for m in (basis_y, basis_y.T, basis_z, basis_z.T, basis_x, basis_x.T)]
    squares_x = np.repeat(wave_squares(first_length)[:, None], third_length, 1).astype(np.float32)
    squares_z = wave_squares(third_length)[None, :].astype(np.float32)

    tiles = image_count * planes * 2 // SUBLANES
    assert tiles * SUBLANES == image_count * planes * 2
    chunk = lambda count: pltpu.VMEM((axis_size, count, SUBLANES, third_length), jnp.float32)
    assert ITERS * (image_count - 1) <= third_length
    vmem = pl.BlockSpec(memory_space=pltpu.VMEM)
    return pl.pallas_call(
        functools.partial(kernel, images.shape, axis_size),
        out_shape=(
            jax.ShapeDtypeStruct(images.shape, jnp.float32),
            jax.ShapeDtypeStruct((ITERS, image_count - 1), jnp.float32),
        ),
        in_specs=[vmem, pl.BlockSpec(memory_space=pltpu.SMEM)] + [vmem] * 8,
        out_specs=(vmem, vmem),
        scratch_shapes=[
            chunk(2 * tiles), chunk(2 * tiles),
            chunk(tiles), chunk(tiles), chunk(tiles), chunk(tiles), chunk(tiles), chunk(tiles),
            pltpu.VMEM((1, 1, third_length), jnp.float32),
            pltpu.VMEM((axis_size, 1, third_length), jnp.float32),
            pltpu.VMEM((first_length, image_count * 2 * third_length), jnp.float32),
            pltpu.SemaphoreType.DMA((5,)),
            pltpu.SemaphoreType.DMA((5,)),
        ],
        compiler_params=pltpu.CompilerParams(collective_id=0, has_side_effects=True, vmem_limit_bytes=32 * 1024 * 1024),
    )(images, weights, *[jnp.asarray(t) for t in tables], jnp.asarray(squares_x), jnp.asarray(squares_z))


def solution(mesh):
    return jax.shard_map(
        functools.partial(local, mesh.shape["space"]),
        mesh=mesh,
        in_specs=(P("group", "space", None, None), P("group", None)),
        out_specs=(P("group", "space", None, None), P("group", None)),
        check_vma=False,
    )
```

time: 341 us -> 176 us (0.52); the launches traced: 335 us -> 175 us
  Pallas kernels: 0 us -> 167 us
  blocking collectives: 166 us -> 0 us
  waiting for transfers between devices: 84.2 us -> 0 us
  starting transfers between devices: 40.4 us -> 0 us
  matrix products: 32.4 us -> 0 us
  other arithmetic: 3.91 us -> 0 us
    pallas_call x0 -> x1, Pallas kernels: none -> 167 us  [local(): pl.pallas_call(functools.partial(kernel, images.shape, axis_size), out_sh...]
    all_to_all x3 -> x0, blocking collectives: 166 us -> none  [the longest x2 97.6 us: local(): lax.all_to_all(partial_value, 'space', split_axis=2, concat_axis=3, tiled...]
    all_to_all x2 -> x0, waiting for transfers between devices: 84.2 us -> none  [the longest x1 63.3 us: local(): lax.all_to_all(spectra, 'space', split_axis=4, concat_axis=3, tiled=True)]
    all_to_all x2 -> x0, starting transfers between devices: 40.4 us -> none  [the longest x1 34.9 us: local(): lax.all_to_all(spectra, 'space', split_axis=4, concat_axis=3, tiled=True)]
    dot_general x50 -> x0, matrix products: 32.4 us -> none  [the longest x16 10.8 us: along_second(): return jnp.einsum('...xyz,ky->...xkz', values, matrix, precision=highest)]
    unnamed x5 -> x17, local copies, waits for them, and re-layouts: 0.74 us -> 7.18 us
  transfers between devices with their start and end apart: 2 -> 0, of which waited for: 2 -> 0; matrix products, arithmetic and copies ran while one was open for 1% -> 0% of each run, Pallas kernels for 0% -> 0%
where the time goes in v1:
time: 176 us; the launch traced here: 175 us
  Pallas kernels  167 us (95%)
  local copies, waits for them, and re-layouts  7.77 us (4%)
    pallas_call x1, Pallas kernels, local(): pl.pallas_call(functools.partial(kernel, images.shape, axis_size), out_sh...  167 us
    unnamed x17, local copies, waits for them, and re-layouts  7.18 us

profile of v1, /device:TPU:37, one launch (start us, length us, event | category | flops | bytes accessed | tf_op | source)
XLA Modules:
  0.0 175.5 jit_solution(15982528451150107747)
XLA Ops:
  0.6 0.0 copy-start.7
  0.6 0.6 copy-done.7
  1.3 0.0 copy-start
  1.3 0.9 copy-done
  2.2 0.0 copy-start.1
  2.2 0.8 copy-done.1
  3.1 0.0 copy-start.2
  3.1 0.8 copy-done.2
  3.9 0.0 copy-start.3
  3.9 0.8 copy-done.3
  4.8 0.0 copy-start.4
  4.8 0.8 copy-done.4
  5.6 0.0 copy-start.5
  5.6 0.8 copy-done.5
  6.4 0.0 copy-start.6
  6.4 0.7 copy-done.6
  7.1 167.1 %shard_map.113 = (f32[2,2,128,128]{3,2,1,0:T(8,128)S(1)}, f32[2,1]{1,0:T(2,128)S(1)}) custom-call(f32[2,2,128,128]{3,2,1,0:T(8,128)S(1)} %copy-done, f32[2,2]{1,0:T(2,128)S(1)} %copy-done.6, bf16[2,128,128]{2,1,0:T(8,128)(2,1)S(1)} %copy-done.2, bf16[2,128,128]{2,1,0:T(8,128)(2,1)S(1)} %copy-done.1, bf16[2,128,128]{2,1,0:T(8,128)(2,1)S(1)} %copy-done.2, ...), custom_call_target="tpu_custom_call" | custom-call | tf_op jit(solution)/shard_map/pallas_call | solution.py:270
  174.2 0.6 copy.12
  174.8 0.7 copy.14
Async XLA Ops:
  0.6 0.7 copy-start.7
  1.3 0.9 copy-start
  2.2 0.8 copy-start.1
  3.1 0.8 copy-start.2
  3.9 0.8 copy-start.3
  4.8 0.8 copy-start.4
  5.6 0.8 copy-start.5
  6.4 0.7 copy-start.6

commit v2 on v1

v2 whole, which is shorter than its diff:
```python
import functools
import math

import jax
import jax.numpy as jnp
import numpy as np
from jax import lax
from jax.experimental import pallas as pl
from jax.experimental.pallas import tpu as pltpu
from jax.sharding import PartitionSpec as P

ITERS = 2
CORES = 2
TABLES = 6
time_step = 0.1
gradient_weight = 1.0


def frequencies(length):
    half = length // 2
    return np.concatenate([np.arange(half), [half], np.arange(1, half)])


def real_basis(length):
    half = length // 2
    cells = np.arange(length)
    product = np.outer(frequencies(length), cells) % length
    angles = product * (2.0 * math.pi / length)
    rows = np.where(np.arange(length)[:, None] <= half, np.cos(angles), np.sin(angles)) * math.sqrt(2.0 / length)
    rows[[0, half]] *= math.sqrt(0.5)
    return rows


def split(value):
    high = value.astype(jnp.bfloat16)
    return high, (value - high.astype(jnp.float32)).astype(jnp.bfloat16)


def product(left, right):
    dot = functools.partial(jnp.dot, preferred_element_type=jnp.float32)
    return dot(left[0], right[0]) + (dot(left[0], right[1]) + dot(left[1], right[0]))


def kernel(
    shape, axis_size,
    images_hbm, weights_hbm, *refs,
):
    tables_hbm, refs = refs[:TABLES], refs[TABLES:]
    out_ref, spacing_ref, images_ref, weights_ref = refs[:4]
    tables, refs = refs[4 : 4 + TABLES], refs[4 + TABLES :]
    (
        first_send, first_recv, back_send, back_recv, next_send, next_recv, last_send, last_recv,
        part_send, part_recv, field_spectrum, load_sem, send_sem, recv_sem,
    ) = refs
    image_count, planes, second_length, third_length = shape
    first_length = planes * axis_size
    half = second_length // 2
    chips = axis_size // CORES
    me = lax.axis_index("space")
    group = lax.axis_index("group")
    my_chip, my_core = me // CORES, lax.rem(me, CORES)
    both = image_count * planes

    def partner(offset, core):
        return lax.rem(my_chip + offset + chips, chips) * CORES + core

    def farthest_first(visit):
        visit(partner(chips // 2, my_core))
        visit(partner(chips // 2, 1 - my_core))

        def step(i, carry):
            distance = chips // 2 - 1 - i
            visit(partner(distance, my_core))
            visit(partner(-distance, my_core))
            visit(partner(distance, 1 - my_core))
            visit(partner(-distance, 1 - my_core))
            return carry

        lax.fori_loop(0, chips // 2 - 1, step, 0)
        visit(partner(0, 1 - my_core))

    barrier = pltpu.get_barrier_semaphore()
    farthest_first(
        lambda target: pl.semaphore_signal(
            barrier, inc=1, device_id=(group, target), device_id_type=pl.DeviceIdType.MESH
        )
    )
    loads = [
        pltpu.make_async_copy(source, target, load_sem.at[i])
        for i, (source, target) in enumerate(
            zip((images_hbm, weights_hbm, *tables_hbm), (images_ref, weights_ref, *tables))
        )
    ]
    for load in loads:
        load.start()

    def exchange(send, recv, rows, phase):
        recv[me, rows] = send[me, rows]

        def copy_to(target):
            pltpu.make_async_remote_copy(
                src_ref=send.at[target, rows],
                dst_ref=recv.at[me, rows],
                send_sem=send_sem.at[phase],
                recv_sem=recv_sem.at[phase],
                device_id=(group, target),
                device_id_type=pl.DeviceIdType.MESH,
            ).start()

        farthest_first(copy_to)

    def finish(recv, rows, phase):
        arrived = recv.at[pl.ds(0, axis_size - 1), rows]
        pltpu.make_async_copy(arrived, arrived, recv_sem.at[phase]).wait()

    def drain(send, rows, phase):
        sent = send.at[pl.ds(0, axis_size - 1), rows]
        pltpu.make_async_copy(sent, sent, send_sem.at[phase]).wait()

    def matrix(k):
        return tables[k][0], tables[k][1]

    qy, qyt, qz, qzt, qx, qxt = [lambda k=k: matrix(k) for k in range(TABLES)]

    def forward_slab(value):
        return product(qy(), split(product(split(value), qzt())))

    def backward_slab(recv, even_row, odd_row):
        spectrum = jnp.concatenate([recv[:, even_row, :], recv[:, odd_row, :]], 0)
        return product(split(product(qyt(), split(spectrum))), qz())

    def pencils(recv, rows):
        return jnp.concatenate([recv[:, row, :] for row in rows], 0)

    def forward_pencils(columns):
        return product(qx(), split(jnp.concatenate(columns, 1)))

    def potential(value):
        return value * value * value - value

    def first_row(parity, field, image, plane):
        return parity * 2 * both + (field * image_count + image) * planes + plane

    def back_row(parity, image, plane):
        return (parity * image_count + image) * planes + plane

    def next_row(image, parity, plane):
        return (image * 2 + parity) * planes + plane

    for load in loads:
        load.wait()
    for image in range(image_count):
        for plane in range(planes):
            value = images_ref[image, plane]
            for field, part in enumerate((value, potential(value))):
                spectrum = forward_slab(part)
                for parity in range(2):
                    first_send[:, first_row(parity, field, image, plane), :] = spectrum[parity * half : (parity + 1) * half]
    pl.semaphore_wait(barrier, axis_size - 1)
    first_rows = [pl.ds(parity * 2 * both, 2 * both) for parity in range(2)]
    for parity in range(2):
        exchange(first_send, first_recv, first_rows[parity], parity)

    def squares_of(index, length):
        frequency = jnp.where(index <= length // 2, index, index - length // 2).astype(jnp.float32)
        number = frequency * (2.0 * math.pi / length)
        return number * number

    square_x = squares_of(lax.broadcasted_iota(jnp.int32, (first_length, third_length), 0), first_length)
    square_z = squares_of(lax.broadcasted_iota(jnp.int32, (first_length, third_length), 1), third_length)
    my_rows = jnp.full((first_length, third_length), me, jnp.int32)
    frequencies_y = (my_rows, jnp.where(my_rows == 0, half, my_rows))
    damping, coupling = [], []
    for frequency in frequencies_y:
        number = frequency.astype(jnp.float32) * (2.0 * math.pi / second_length)
        squares = square_x + number * number + square_z
        damping.append(1.0 / (1.0 + time_step * gradient_weight * squares * squares))
        coupling.append(time_step * squares * damping[-1])

    weight = [[weights_ref[i : i + 1, j : j + 1] for j in range(image_count)] for i in range(image_count)]

    def mixed(values):
        new = []
        for i in range(image_count):
            total = weight[i][0] * values[0]
            for j in range(1, image_count):
                total = total + weight[i][j] * values[j]
            new.append(total)
        return new

    def columns_of(value, k):
        return value[:, k * third_length : (k + 1) * third_length]

    lane = lax.broadcasted_iota(jnp.int32, (1, third_length), 1)

    def spacing_parts(values, row, iteration):
        for j in range(image_count - 1):
            difference = values[j + 1] - values[j]
            row = row + jnp.where(lane == iteration * (image_count - 1) + j, jnp.sum(difference * difference), 0.0)
        return row

    parts = jnp.zeros((1, third_length), jnp.float32)
    back_chunks = [(0, pl.ds(0, both), 2)] + [
        (1, pl.ds(both + image * planes, planes), 3 + image) for image in range(image_count)
    ]
    for parity in range(2):
        finish(first_recv, first_rows[parity], parity)
        spectra = forward_pencils([
            pencils(first_recv, [first_row(parity, field, image, plane) for plane in range(planes)])
            for field in range(2)
            for image in range(image_count)
        ])
        new = [
            damping[parity] * columns_of(spectra, image) - coupling[parity] * columns_of(spectra, image_count + image)
            for image in range(image_count)
        ]
        parts = spacing_parts(new, parts, 0)
        new = mixed(new)
        for image in range(image_count):
            field_spectrum[image, parity] = new[image]
        values = product(qxt(), split(jnp.concatenate(new, 1)))
        for image in range(image_count):
            for plane in range(planes):
                back_send[:, back_row(parity, image, plane), :] = columns_of(values, image)[
                    plane * axis_size : (plane + 1) * axis_size
                ]
        for chunk_parity, rows, phase in back_chunks:
            if chunk_parity == parity:
                exchange(back_send, back_recv, rows, phase)

    image_rows = [pl.ds(image * 2 * planes, 2 * planes) for image in range(image_count)]
    finish(back_recv, back_chunks[0][1], back_chunks[0][2])
    for image in range(image_count):
        finish(back_recv, back_chunks[1 + image][1], back_chunks[1 + image][2])
        for plane in range(planes):
            value = backward_slab(back_recv, back_row(0, image, plane), back_row(1, image, plane))
            spectrum = forward_slab(potential(value))
            for parity in range(2):
                next_send[:, next_row(image, parity, plane), :] = spectrum[parity * half : (parity + 1) * half]
        exchange(next_send, next_recv, image_rows[image], 3 + image_count + image)

    part_phase = 3 + 3 * image_count
    spectra = []
    for image in range(image_count):
        finish(next_recv, image_rows[image], 3 + image_count + image)
        changes = forward_pencils([
            pencils(next_recv, [next_row(image, parity, plane) for plane in range(planes)]) for parity in range(2)
        ])
        new = [
            damping[parity] * field_spectrum[image, parity] - coupling[parity] * columns_of(changes, parity)
            for parity in range(2)
        ]
        new = jnp.concatenate(new, 1)
        spectra.append(new)
        if image == image_count - 1:
            part_send[0] = spacing_parts(spectra, parts, 1)
            part_recv[me] = part_send[0]
            farthest_first(
                lambda target: pltpu.make_async_remote_copy(
                    src_ref=part_send.at[0],
                    dst_ref=part_recv.at[me],
                    send_sem=send_sem.at[part_phase],
                    recv_sem=recv_sem.at[part_phase],
                    device_id=(group, target),
                    device_id_type=pl.DeviceIdType.MESH,
                ).start()
            )
        values = product(qxt(), split(new))
        for parity in range(2):
            for plane in range(planes):
                last_send[:, next_row(image, parity, plane), :] = columns_of(values, parity)[
                    plane * axis_size : (plane + 1) * axis_size
                ]
        exchange(last_send, last_recv, image_rows[image], 3 + 2 * image_count + image)

    relaxed = []
    for image in range(image_count):
        if image == image_count - 1:
            arrived = part_recv.at[pl.ds(0, axis_size - 1)]
            pltpu.make_async_copy(arrived, arrived, recv_sem.at[part_phase]).wait()
            cell_count = first_length * second_length * third_length
            totals = jnp.sum(part_recv[...], axis=0) / cell_count
            spacing_ref[...] = totals[:, : ITERS * (image_count - 1)]
        finish(last_recv, image_rows[image], 3 + 2 * image_count + image)
        relaxed.append([
            backward_slab(last_recv, next_row(image, 0, plane), next_row(image, 1, plane)) for plane in range(planes)
        ])
    for plane in range(planes):
        for image, value in enumerate(mixed([relaxed[j][plane] for j in range(image_count)])):
            out_ref[image, plane] = value

    for parity in range(2):
        drain(first_send, first_rows[parity], parity)
    for _, rows, phase in back_chunks:
        drain(back_send, rows, phase)
    for image in range(image_count):
        drain(next_send, image_rows[image], 3 + image_count + image)
        drain(last_send, image_rows[image], 3 + 2 * image_count + image)
    sent = part_recv.at[pl.ds(0, axis_size - 1)]
    pltpu.make_async_copy(sent, sent, send_sem.at[part_phase]).wait()


def two_parts(matrix):
    matrix = matrix.astype(np.float32)
    high = matrix.astype(jnp.bfloat16)
    low = (matrix - high.astype(np.float32)).astype(jnp.bfloat16)
    return np.stack([high, low])


def local(axis_size, images, weights):
    image_count, planes, second_length, third_length = images.shape
    first_length = planes * axis_size
    assert second_length == 2 * axis_size and axis_size % (2 * CORES) == 0
    assert ITERS * (image_count - 1) <= third_length
    basis_x = real_basis(first_length)
    order = np.arange(first_length).reshape(axis_size, planes).T.reshape(-1)
    basis_x = basis_x[:, order]
    basis_y, basis_z = real_basis(second_length), real_basis(third_length)
    tables = [two_parts(m) for m in (basis_y, basis_y.T, basis_z, basis_z.T, basis_x, basis_x.T)]

    rows = image_count * planes * 2
    message = lambda count: pltpu.VMEM((axis_size, count, third_length), jnp.float32)
    phases = 4 + 3 * image_count
    hbm = pl.BlockSpec(memory_space=pltpu.HBM)
    vmem = pl.BlockSpec(memory_space=pltpu.VMEM)
    relaxed, spacing = pl.pallas_call(
        functools.partial(kernel, images.shape, axis_size),
        out_shape=(
            jax.ShapeDtypeStruct(images.shape, jnp.float32),
            jax.ShapeDtypeStruct((1, ITERS * (image_count - 1)), jnp.float32),
        ),
        in_specs=[hbm] * (2 + TABLES),
        out_specs=(vmem, vmem),
        scratch_shapes=[
            pltpu.VMEM(images.shape, jnp.float32),
            pltpu.VMEM(weights.shape, jnp.float32),
            *[pltpu.VMEM(t.shape, jnp.bfloat16) for t in tables],
            message(2 * rows), message(2 * rows),
            message(rows), message(rows), message(rows), message(rows), message(rows), message(rows),
            message(1), message(1),
            pltpu.VMEM((image_count, 2, first_length, third_length), jnp.float32),
            pltpu.SemaphoreType.DMA((2 + TABLES,)),
            pltpu.SemaphoreType.DMA((phases,)),
            pltpu.SemaphoreType.DMA((phases,)),
        ],
        compiler_params=pltpu.CompilerParams(collective_id=0, has_side_effects=True),
    )(images, weights, *[jnp.asarray(t) for t in tables])
    return relaxed, spacing.reshape(ITERS, image_count - 1)


def solution(mesh):
    return jax.shard_map(
        functools.partial(local, mesh.shape["space"]),
        mesh=mesh,
        in_specs=(P("group", "space", None, None), P("group", None)),
        out_specs=(P("group", "space", None, None), P("group", None)),
        check_vma=False,
    )
```

time: 176 us -> 160 us (0.909)
  Pallas kernels: 167 us -> 157 us
  local copies, waits for them, and re-layouts: 7.77 us -> 2.19 us
    pallas_call x1, Pallas kernels: 167 us -> 157 us  [local(): pl.pallas_call(functools.partial(kernel, images.shape, axis_size), out_sh...]
    unnamed x17 -> x4, local copies, waits for them, and re-layouts: 7.18 us -> 2.19 us
where the time goes in v2:
time: 160 us
  Pallas kernels  157 us (98%)
  local copies, waits for them, and re-layouts  2.19 us (1%)
    pallas_call x1, Pallas kernels, local(): pl.pallas_call(functools.partial(kernel, images.shape, axis_size), out_sh...  157 us

profile of v2, /device:TPU:37, one launch (start us, length us, event | category | flops | bytes accessed | tf_op | source)
XLA Modules:
  0.0 160.1 jit_solution(14741338359723521362)
XLA Ops:
  0.6 157.2 %shard_map.95 = (f32[2,2,128,128]{3,2,1,0:T(8,128)}, f32[1,2]{1,0:T(1,128)}) custom-call(f32[2,2,128,128]{3,2,1,0:T(8,128)} %images_hbm.1, f32[2,2]{1,0:T(2,128)} %weights_hbm.1, bf16[2,128,128]{2,1,0:T(8,128)(2,1)} %constant.8.clone.refs_0_.refs_2_, bf16[2,128,128]{2,1,0:T(8,128)(2,1)} %constant.9.clone.refs_1_.refs_3_, ...), custom_call_target="tpu_custom_call" | custom-call | tf_op jit(solution)/shard_map/pallas_call | solution.py:326
  157.9 0.0 copy-start
  157.9 1.7 %copy.12 = f32[2,2,128,128]{3,2,1,0:T(8,128)} copy(f32[2,2,128,128]{3,2,1,0:T(8,128)} %get-tuple-element.8) | data formatting | bytes 524288
  159.6 0.0 copy-done
  159.6 0.5 copy.13
Async XLA Ops:
  157.9 1.7 %copy-start = (f32[1,2]{1,0:T(1,128)S(1)}, f32[1,2]{1,0:T(1,128)}, u32[]{:S(2)}) copy-start(f32[1,2]{1,0:T(1,128)} %get-tuple-element.5) | copy-start | bytes 28

commit v3 on v2

--- a/solution.py
+++ b/solution.py
@@ -50,7 +50,7 @@
     tables, refs = refs[4 : 4 + TABLES], refs[4 + TABLES :]
     (
         first_send, first_recv, back_send, back_recv, next_send, next_recv, last_send, last_recv,
-        part_send, part_recv, field_spectrum, load_sem, send_sem, recv_sem,
+        pair_send, pair_recv, part_send, part_recv, field_spectrum, load_sem, send_sem, recv_sem,
     ) = refs
     image_count, planes, second_length, third_length = shape
     first_length = planes * axis_size
@@ -141,10 +141,7 @@
     def first_row(parity, field, image, plane):
         return parity * 2 * both + (field * image_count + image) * planes + plane
 
-    def back_row(parity, image, plane):
-        return (parity * image_count + image) * planes + plane
-
-    def next_row(image, parity, plane):
+    def row_of(image, parity, plane):
         return (image * 2 + parity) * planes + plane
 
     for load in loads:
@@ -200,8 +197,8 @@
         return row
 
     parts = jnp.zeros((1, third_length), jnp.float32)
-    back_chunks = [(0, pl.ds(0, both), 2)] + [
-        (1, pl.ds(both + image * planes, planes), 3 + image) for image in range(image_count)
+    back_chunks = [(0, pl.ds(0, planes), 2), (1, pl.ds(planes, planes), 3)] + [
+        (1, pl.ds(image * 2 * planes, 2 * planes), 3 + image) for image in range(1, image_count)
     ]
     for parity in range(2):
         finish(first_recv, first_rows[parity], parity)
@@ -221,7 +218,7 @@
         values = product(qxt(), split(jnp.concatenate(new, 1)))
         for image in range(image_count):
             for plane in range(planes):
-                back_send[:, back_row(parity, image, plane), :] = columns_of(values, image)[
+                back_send[:, row_of(image, parity, plane), :] = columns_of(values, image)[
                     plane * axis_size : (plane + 1) * axis_size
                 ]
         for chunk_parity, rows, phase in back_chunks:
@@ -233,10 +230,10 @@
     for image in range(image_count):
         finish(back_recv, back_chunks[1 + image][1], back_chunks[1 + image][2])
         for plane in range(planes):
-            value = backward_slab(back_recv, back_row(0, image, plane), back_row(1, image, plane))
+            value = backward_slab(back_recv, row_of(image, 0, plane), row_of(image, 1, plane))
             spectrum = forward_slab(potential(value))
             for parity in range(2):
-                next_send[:, next_row(image, parity, plane), :] = spectrum[parity * half : (parity + 1) * half]
+                next_send[:, row_of(image, parity, plane), :] = spectrum[parity * half : (parity + 1) * half]
         exchange(next_send, next_recv, image_rows[image], 3 + image_count + image)
 
     part_phase = 3 + 3 * image_count
@@ -244,7 +241,7 @@
     for image in range(image_count):
         finish(next_recv, image_rows[image], 3 + image_count + image)
         changes = forward_pencils([
-            pencils(next_recv, [next_row(image, parity, plane) for plane in range(planes)]) for parity in range(2)
+            pencils(next_recv, [row_of(image, parity, plane) for plane in range(planes)]) for parity in range(2)
         ])
         new = [
             damping[parity] * field_spectrum[image, parity] - coupling[parity] * columns_of(changes, parity)
@@ -253,37 +250,52 @@
         new = jnp.concatenate(new, 1)
         spectra.append(new)
         if image == image_count - 1:
-            part_send[0] = spacing_parts(spectra, parts, 1)
-            part_recv[me] = part_send[0]
-            farthest_first(
-                lambda target: pltpu.make_async_remote_copy(
-                    src_ref=part_send.at[0],
-                    dst_ref=part_recv.at[me],
-                    send_sem=send_sem.at[part_phase],
-                    recv_sem=recv_sem.at[part_phase],
-                    device_id=(group, target),
-                    device_id_type=pl.DeviceIdType.MESH,
-                ).start()
+            pair_send[...] = spacing_parts(spectra, parts, 1)
+            to_other_core = pltpu.make_async_remote_copy(
+                src_ref=pair_send,
+                dst_ref=pair_recv,
+                send_sem=send_sem.at[part_phase + 1],
+                recv_sem=recv_sem.at[part_phase + 1],
+                device_id=(group, partner(0, 1 - my_core)),
+                device_id_type=pl.DeviceIdType.MESH,
             )
+            to_other_core.start()
         values = product(qxt(), split(new))
         for parity in range(2):
             for plane in range(planes):
-                last_send[:, next_row(image, parity, plane), :] = columns_of(values, parity)[
+                last_send[:, row_of(image, parity, plane), :] = columns_of(values, parity)[
                     plane * axis_size : (plane + 1) * axis_size
                 ]
+        if image == image_count - 1:
+            to_other_core.wait()
+            part_send[...] = pair_send[...] + pair_recv[...]
+            part_recv[my_chip] = part_send[...]
+
+            def part_to(step, carry):
+                pltpu.make_async_remote_copy(
+                    src_ref=part_send,
+                    dst_ref=part_recv.at[my_chip],
+                    send_sem=send_sem.at[part_phase],
+                    recv_sem=recv_sem.at[part_phase],
+                    device_id=(group, partner(step, my_core)),
+                    device_id_type=pl.DeviceIdType.MESH,
+                ).start()
+                return carry
+
+            lax.fori_loop(1, chips, part_to, 0)
         exchange(last_send, last_recv, image_rows[image], 3 + 2 * image_count + image)
 
     relaxed = []
     for image in range(image_count):
         if image == image_count - 1:
-            arrived = part_recv.at[pl.ds(0, axis_size - 1)]
+            arrived = part_recv.at[pl.ds(0, chips - 1)]
             pltpu.make_async_copy(arrived, arrived, recv_sem.at[part_phase]).wait()
             cell_count = first_length * second_length * third_length
             totals = jnp.sum(part_recv[...], axis=0) / cell_count
             spacing_ref[...] = totals[:, : ITERS * (image_count - 1)]
         finish(last_recv, image_rows[image], 3 + 2 * image_count + image)
         relaxed.append([
-            backward_slab(last_recv, next_row(image, 0, plane), next_row(image, 1, plane)) for plane in range(planes)
+            backward_slab(last_recv, row_of(image, 0, plane), row_of(image, 1, plane)) for plane in range(planes)
         ])
     for plane in range(planes):
         for image, value in enumerate(mixed([relaxed[j][plane] for j in range(image_count)])):
@@ -296,7 +308,7 @@
     for image in range(image_count):
         drain(next_send, image_rows[image], 3 + image_count + image)
         drain(last_send, image_rows[image], 3 + 2 * image_count + image)
-    sent = part_recv.at[pl.ds(0, axis_size - 1)]
+    sent = part_recv.at[pl.ds(0, chips - 1)]
     pltpu.make_async_copy(sent, sent, send_sem.at[part_phase]).wait()
 
 
@@ -320,14 +332,15 @@
 
     rows = image_count * planes * 2
     message = lambda count: pltpu.VMEM((axis_size, count, third_length), jnp.float32)
-    phases = 4 + 3 * image_count
+    row = pltpu.VMEM((1, third_length), jnp.float32)
+    phases = 5 + 3 * image_count
     hbm = pl.BlockSpec(memory_space=pltpu.HBM)
     vmem = pl.BlockSpec(memory_space=pltpu.VMEM)
     relaxed, spacing = pl.pallas_call(
         functools.partial(kernel, images.shape, axis_size),
         out_shape=(
-            jax.ShapeDtypeStruct(images.shape, jnp.float32),
-            jax.ShapeDtypeStruct((1, ITERS * (image_count - 1)), jnp.float32),
+            pltpu.VMEM(images.shape, jnp.float32),
+            pltpu.VMEM((1, ITERS * (image_count - 1)), jnp.float32),
         ),
         in_specs=[hbm] * (2 + TABLES),
         out_specs=(vmem, vmem),
@@ -337,7 +350,7 @@
             *[pltpu.VMEM(t.shape, jnp.bfloat16) for t in tables],
             message(2 * rows), message(2 * rows),
             message(rows), message(rows), message(rows), message(rows), message(rows), message(rows),
-            message(1), message(1),
+            row, row, row, pltpu.VMEM((axis_size // CORES, 1, third_length), jnp.float32),
             pltpu.VMEM((image_count, 2, first_length, third_length), jnp.float32),
             pltpu.SemaphoreType.DMA((2 + TABLES,)),
             pltpu.SemaphoreType.DMA((phases,)),

time: 160 us -> 152 us (0.950)
  Pallas kernels: 157 us -> 151 us
    pallas_call x1, Pallas kernels: 157 us -> 151 us  [local(): pl.pallas_call(functools.partial(kernel, images.shape, axis_size), out_sh...]
where the time goes in v3:
time: 152 us
  Pallas kernels  151 us (99%)
    pallas_call x1, Pallas kernels, local(): pl.pallas_call(functools.partial(kernel, images.shape, axis_size), out_sh...  151 us

profile of v3, /device:TPU:37, one launch (start us, length us, event | category | flops | bytes accessed | tf_op | source)
XLA Modules:
  0.0 152.4 jit_solution(1988186358414683248)
XLA Ops:
  0.6 150.5 %shard_map.95 = (f32[2,2,128,128]{3,2,1,0:T(8,128)S(1)}, f32[1,2]{1,0:T(1,128)S(1)}) custom-call(f32[2,2,128,128]{3,2,1,0:T(8,128)} %images_hbm.1, f32[2,2]{1,0:T(2,128)} %weights_hbm.1, bf16[2,128,128]{2,1,0:T(8,128)(2,1)} %constant.8.clone.refs_0_.refs_2_, bf16[2,128,128]{2,1,0:T(8,128)(2,1)} %constant.9.clone.refs_1_.refs_3_, ...), custom_call_target="tpu_custom_call" | custom-call | tf_op jit(solution)/shard_map/pallas_call | solution.py:339
  151.2 0.7 copy.12
  151.9 0.5 copy.13

commit v4 on v3

--- a/solution.py
+++ b/solution.py
@@ -50,7 +50,7 @@
     tables, refs = refs[4 : 4 + TABLES], refs[4 + TABLES :]
     (
         first_send, first_recv, back_send, back_recv, next_send, next_recv, last_send, last_recv,
-        pair_send, pair_recv, part_send, part_recv, field_spectrum, load_sem, send_sem, recv_sem,
+        pair_send, pair_recv, part_send, part_recv, field_spectrum, load_sem, send_sem, recv_sem, ready_sem,
     ) = refs
     image_count, planes, second_length, third_length = shape
     first_length = planes * axis_size
@@ -79,12 +79,6 @@
         lax.fori_loop(0, chips // 2 - 1, step, 0)
         visit(partner(0, 1 - my_core))
 
-    barrier = pltpu.get_barrier_semaphore()
-    farthest_first(
-        lambda target: pl.semaphore_signal(
-            barrier, inc=1, device_id=(group, target), device_id_type=pl.DeviceIdType.MESH
-        )
-    )
     loads = [
         pltpu.make_async_copy(source, target, load_sem.at[i])
         for i, (source, target) in enumerate(
@@ -94,9 +88,14 @@
     for load in loads:
         load.start()
 
-    def exchange(send, recv, rows, phase):
-        recv[me, rows] = send[me, rows]
-
+    def signal(semaphore, target):
+        pl.semaphore_signal(semaphore, inc=1, device_id=(group, target), device_id_type=pl.DeviceIdType.MESH)
+
+    neighbours = [(0, 1 - my_core)] + [(offset, core) for offset in (1, -1) for core in (my_core, 1 - my_core)]
+    barrier = pltpu.get_barrier_semaphore()
+    for offset, core in neighbours:
+        signal(barrier, partner(offset, core))
+    def sender(send, recv, rows, phase):
         def copy_to(target):
             pltpu.make_async_remote_copy(
                 src_ref=send.at[target, rows],
@@ -107,7 +106,41 @@
                 device_id_type=pl.DeviceIdType.MESH,
             ).start()
 
-        farthest_first(copy_to)
+        return copy_to
+
+    def exchange(send, recv, rows, phase):
+        recv[me, rows] = send[me, rows]
+        farthest_first(sender(send, recv, rows, phase))
+
+    def opening_exchange(send, recv, rows, phase):
+        copy_to = sender(send, recv, rows, phase)
+        recv[me, rows] = send[me, rows]
+        pl.semaphore_wait(barrier, len(neighbours))
+
+        def tell():
+            signal(ready_sem.at[0], partner(1, my_core))
+            signal(ready_sem.at[1], partner(-1, my_core))
+
+        def hear():
+            for side in range(2):
+                pl.semaphore_wait(ready_sem.at[side], 1)
+
+        tell()
+        for offset, core in neighbours:
+            copy_to(partner(offset, core))
+
+        def step(distance, carry):
+            hear()
+            tell()
+            for core in (my_core, 1 - my_core):
+                copy_to(partner(distance, core))
+                copy_to(partner(-distance, core))
+            return carry
+
+        lax.fori_loop(2, chips // 2, step, 0)
+        hear()
+        for core in (my_core, 1 - my_core):
+            copy_to(partner(chips // 2, core))
 
     def finish(recv, rows, phase):
         arrived = recv.at[pl.ds(0, axis_size - 1), rows]
@@ -153,10 +186,9 @@
                 spectrum = forward_slab(part)
                 for parity in range(2):
                     first_send[:, first_row(parity, field, image, plane), :] = spectrum[parity * half : (parity + 1) * half]
-    pl.semaphore_wait(barrier, axis_size - 1)
     first_rows = [pl.ds(parity * 2 * both, 2 * both) for parity in range(2)]
-    for parity in range(2):
-        exchange(first_send, first_recv, first_rows[parity], parity)
+    opening_exchange(first_send, first_recv, first_rows[0], 0)
+    exchange(first_send, first_recv, first_rows[1], 1)
 
     def squares_of(index, length):
         frequency = jnp.where(index <= length // 2, index, index - length // 2).astype(jnp.float32)
@@ -322,7 +354,7 @@
 def local(axis_size, images, weights):
     image_count, planes, second_length, third_length = images.shape
     first_length = planes * axis_size
-    assert second_length == 2 * axis_size and axis_size % (2 * CORES) == 0
+    assert second_length == 2 * axis_size and axis_size % (2 * CORES) == 0 and axis_size > 4 * CORES
     assert ITERS * (image_count - 1) <= third_length
     basis_x = real_basis(first_length)
     order = np.arange(first_length).reshape(axis_size, planes).T.reshape(-1)
@@ -355,6 +387,7 @@
             pltpu.SemaphoreType.DMA((2 + TABLES,)),
             pltpu.SemaphoreType.DMA((phases,)),
             pltpu.SemaphoreType.DMA((phases,)),
+            pltpu.SemaphoreType.REGULAR((2,)),
         ],
         compiler_params=pltpu.CompilerParams(collective_id=0, has_side_effects=True),
     )(images, weights, *[jnp.asarray(t) for t in tables])

time: 152 us -> 151 us (level)
  Pallas kernels: 151 us -> 149 us
where the time goes in v4:
time: 151 us
  Pallas kernels  149 us (99%)
    pallas_call x1, Pallas kernels, local(): pl.pallas_call(functools.partial(kernel, images.shape, axis_size), out_sh...  149 us

profile of v4, /device:TPU:37, one launch (start us, length us, event | category | flops | bytes accessed | tf_op | source)
XLA Modules:
  0.0 150.9 jit_solution(2407565756853731828)
XLA Ops:
  0.6 149.0 %shard_map.95 = (f32[2,2,128,128]{3,2,1,0:T(8,128)S(1)}, f32[1,2]{1,0:T(1,128)S(1)}) custom-call(f32[2,2,128,128]{3,2,1,0:T(8,128)} %images_hbm.1, f32[2,2]{1,0:T(2,128)} %weights_hbm.1, bf16[2,128,128]{2,1,0:T(8,128)(2,1)} %constant.8.clone.refs_0_.refs_2_, bf16[2,128,128]{2,1,0:T(8,128)(2,1)} %constant.9.clone.refs_1_.refs_3_, ...), custom_call_target="tpu_custom_call" | custom-call | tf_op jit(solution)/shard_map/pallas_call | solution.py:371
  149.6 0.7 copy.12
  150.3 0.5 copy.13

commit v5 on v3

--- a/solution.py
+++ b/solution.py
@@ -12,6 +12,7 @@
 ITERS = 2
 CORES = 2
 TABLES = 6
+NEAR = 6
 time_step = 0.1
 gradient_weight = 1.0
 
@@ -50,7 +51,7 @@
     tables, refs = refs[4 : 4 + TABLES], refs[4 + TABLES :]
     (
         first_send, first_recv, back_send, back_recv, next_send, next_recv, last_send, last_recv,
-        pair_send, pair_recv, part_send, part_recv, field_spectrum, load_sem, send_sem, recv_sem,
+        pair_send, pair_recv, part_send, part_recv, field_spectrum, load_sem, send_sem, recv_sem, told_sem,
     ) = refs
     image_count, planes, second_length, third_length = shape
     first_length = planes * axis_size
@@ -64,7 +65,9 @@
     def partner(offset, core):
         return lax.rem(my_chip + offset + chips, chips) * CORES + core
 
-    def farthest_first(visit):
+    near = min(NEAR, chips // 2 - 1)
+
+    def farthest_first(visit, beyond=-1):
         visit(partner(chips // 2, my_core))
         visit(partner(chips // 2, 1 - my_core))
 
@@ -76,15 +79,10 @@
             visit(partner(-distance, 1 - my_core))
             return carry
 
-        lax.fori_loop(0, chips // 2 - 1, step, 0)
-        visit(partner(0, 1 - my_core))
-
-    barrier = pltpu.get_barrier_semaphore()
-    farthest_first(
-        lambda target: pl.semaphore_signal(
-            barrier, inc=1, device_id=(group, target), device_id_type=pl.DeviceIdType.MESH
-        )
-    )
+        lax.fori_loop(0, chips // 2 - 1 - max(beyond, 0), step, 0)
+        if beyond < 0:
+            visit(partner(0, 1 - my_core))
+
     loads = [
         pltpu.make_async_copy(source, target, load_sem.at[i])
         for i, (source, target) in enumerate(
@@ -94,9 +92,29 @@
     for load in loads:
         load.start()
 
-    def exchange(send, recv, rows, phase):
-        recv[me, rows] = send[me, rows]
-
+    barrier = pltpu.get_barrier_semaphore()
+
+    def signal(semaphore, target):
+        pl.semaphore_signal(semaphore, inc=1, device_id=(group, target), device_id_type=pl.DeviceIdType.MESH)
+
+    def greet(distance, core):
+        signal(barrier, partner(distance, core))
+        signal(barrier, partner(-distance, core))
+
+    def greet_far(i, carry):
+        greet(chips // 2 - 1 - i, 1)
+        return carry
+
+    def greet_near(i, carry):
+        greet(1 + i, 0)
+        greet(1 + i, 1)
+        return carry
+
+    signal(barrier, partner(chips // 2, 1))
+    lax.fori_loop(0, chips // 2 - 1 - near, greet_far, 0)
+    lax.fori_loop(0, near, greet_near, 0)
+    signal(barrier, partner(0, 1 - my_core))
+    def sender(send, recv, rows, phase):
         def copy_to(target):
             pltpu.make_async_remote_copy(
                 src_ref=send.at[target, rows],
@@ -107,7 +125,11 @@
                 device_id_type=pl.DeviceIdType.MESH,
             ).start()
 
-        farthest_first(copy_to)
+        return copy_to
+
+    def exchange(send, recv, rows, phase, beyond=-1):
+        recv[me, rows] = send[me, rows]
+        farthest_first(sender(send, recv, rows, phase), beyond)
 
     def finish(recv, rows, phase):
         arrived = recv.at[pl.ds(0, axis_size - 1), rows]
@@ -153,10 +175,39 @@
                 spectrum = forward_slab(part)
                 for parity in range(2):
                     first_send[:, first_row(parity, field, image, plane), :] = spectrum[parity * half : (parity + 1) * half]
-    pl.semaphore_wait(barrier, axis_size - 1)
     first_rows = [pl.ds(parity * 2 * both, 2 * both) for parity in range(2)]
-    for parity in range(2):
-        exchange(first_send, first_recv, first_rows[parity], parity)
+
+    @pl.when(my_core == 0)
+    def _():
+        pl.semaphore_wait(barrier, 2 * CORES * near + 1)
+        signal(told_sem.at[0], partner(0, 1))
+
+    @pl.when(my_core == 1)
+    def _():
+        pl.semaphore_wait(told_sem.at[0], 1)
+
+    copy_early = sender(first_send, first_recv, first_rows[0], 0)
+    copy_early(partner(0, 1 - my_core))
+
+    def near_step(i, carry):
+        for core in (my_core, 1 - my_core):
+            copy_early(partner(near - i, core))
+            copy_early(partner(i - near, core))
+        return carry
+
+    lax.fori_loop(0, near, near_step, 0)
+
+    @pl.when(my_core == 1)
+    def _():
+        pl.semaphore_wait(barrier, axis_size - 1)
+        signal(told_sem.at[1], partner(0, 0))
+
+    @pl.when(my_core == 0)
+    def _():
+        pl.semaphore_wait(told_sem.at[1], 1)
+
+    exchange(first_send, first_recv, first_rows[0], 0, near)
+    exchange(first_send, first_recv, first_rows[1], 1)
 
     def squares_of(index, length):
         frequency = jnp.where(index <= length // 2, index, index - length // 2).astype(jnp.float32)
@@ -355,6 +406,7 @@
             pltpu.SemaphoreType.DMA((2 + TABLES,)),
             pltpu.SemaphoreType.DMA((phases,)),
             pltpu.SemaphoreType.DMA((phases,)),
+            pltpu.SemaphoreType.REGULAR((2,)),
         ],
         compiler_params=pltpu.CompilerParams(collective_id=0, has_side_effects=True),
     )(images, weights, *[jnp.asarray(t) for t in tables])

time: 152 us -> 150 us (0.987)
  Pallas kernels: 151 us -> 148 us
    pallas_call x1, Pallas kernels: 151 us -> 148 us  [local(): pl.pallas_call(functools.partial(kernel, images.shape, axis_size), out_sh...]
where the time goes in v5:
time: 150 us; the launch traced here: 149 us
  Pallas kernels  148 us (99%)
    pallas_call x1, Pallas kernels, local(): pl.pallas_call(functools.partial(kernel, images.shape, axis_size), out_sh...  148 us

profile of v5, /device:TPU:37, one launch (start us, length us, event | category | flops | bytes accessed | tf_op | source)
XLA Modules:
  0.0 149.4 jit_solution(3643702541050898635)
XLA Ops:
  0.6 147.6 %shard_map.95 = (f32[2,2,128,128]{3,2,1,0:T(8,128)S(1)}, f32[1,2]{1,0:T(1,128)S(1)}) custom-call(f32[2,2,128,128]{3,2,1,0:T(8,128)} %images_hbm.1, f32[2,2]{1,0:T(2,128)} %weights_hbm.1, bf16[2,128,128]{2,1,0:T(8,128)(2,1)} %constant.8.clone.refs_0_.refs_2_, bf16[2,128,128]{2,1,0:T(8,128)(2,1)} %constant.9.clone.refs_1_.refs_3_, ...), custom_call_target="tpu_custom_call" | custom-call | tf_op jit(solution)/shard_map/pallas_call | solution.py:390
  148.2 0.7 copy.12
  148.9 0.5 copy.13

commit v6 on v5

--- a/solution.py
+++ b/solution.py
@@ -51,7 +51,7 @@
     tables, refs = refs[4 : 4 + TABLES], refs[4 + TABLES :]
     (
         first_send, first_recv, back_send, back_recv, next_send, next_recv, last_send, last_recv,
-        pair_send, pair_recv, part_send, part_recv, field_spectrum, load_sem, send_sem, recv_sem, told_sem,
+        pair_send, pair_recv, total_send, total_recv, part_send, part_recv, field_spectrum, load_sem, send_sem, recv_sem, told_sem,
     ) = refs
     image_count, planes, second_length, third_length = shape
     first_length = planes * axis_size
@@ -320,30 +320,47 @@
         if image == image_count - 1:
             to_other_core.wait()
             part_send[...] = pair_send[...] + pair_recv[...]
-            part_recv[my_chip] = part_send[...]
+
+            @pl.when(my_core == 0)
+            def _():
+                part_recv[0] = part_send[...]
 
             def part_to(step, carry):
                 pltpu.make_async_remote_copy(
                     src_ref=part_send,
-                    dst_ref=part_recv.at[my_chip],
+                    dst_ref=part_recv.at[step],
                     send_sem=send_sem.at[part_phase],
                     recv_sem=recv_sem.at[part_phase],
-                    device_id=(group, partner(step, my_core)),
+                    device_id=(group, partner(CORES * step + my_core, my_core)),
                     device_id_type=pl.DeviceIdType.MESH,
                 ).start()
                 return carry
 
-            lax.fori_loop(1, chips, part_to, 0)
+            lax.fori_loop(1 - my_core, chips // CORES, part_to, 0)
         exchange(last_send, last_recv, image_rows[image], 3 + 2 * image_count + image)
+
+    def wait_parts(semaphores):
+        for core in range(CORES):
+
+            @pl.when(my_core == core)
+            def _():
+                rows = part_recv.at[pl.ds(0, chips // CORES - 1 + core)]
+                pltpu.make_async_copy(rows, rows, semaphores.at[part_phase]).wait()
 
     relaxed = []
     for image in range(image_count):
         if image == image_count - 1:
-            arrived = part_recv.at[pl.ds(0, chips - 1)]
-            pltpu.make_async_copy(arrived, arrived, recv_sem.at[part_phase]).wait()
-            cell_count = first_length * second_length * third_length
-            totals = jnp.sum(part_recv[...], axis=0) / cell_count
-            spacing_ref[...] = totals[:, : ITERS * (image_count - 1)]
+            wait_parts(recv_sem)
+            total_send[...] = jnp.sum(part_recv[...], axis=0)
+            total_to_other_core = pltpu.make_async_remote_copy(
+                src_ref=total_send,
+                dst_ref=total_recv,
+                send_sem=send_sem.at[part_phase + 2],
+                recv_sem=recv_sem.at[part_phase + 2],
+                device_id=(group, partner(0, 1 - my_core)),
+                device_id_type=pl.DeviceIdType.MESH,
+            )
+            total_to_other_core.start()
         finish(last_recv, image_rows[image], 3 + 2 * image_count + image)
         relaxed.append([
             backward_slab(last_recv, row_of(image, 0, plane), row_of(image, 1, plane)) for plane in range(planes)
@@ -359,8 +376,11 @@
     for image in range(image_count):
         drain(next_send, image_rows[image], 3 + image_count + image)
         drain(last_send, image_rows[image], 3 + 2 * image_count + image)
-    sent = part_recv.at[pl.ds(0, chips - 1)]
-    pltpu.make_async_copy(sent, sent, send_sem.at[part_phase]).wait()
+    wait_parts(send_sem)
+    total_to_other_core.wait()
+    cell_count = first_length * second_length * third_length
+    totals = (total_send[...] + total_recv[...]) / cell_count
+    spacing_ref[...] = totals[:, : ITERS * (image_count - 1)]
 
 
 def two_parts(matrix):
@@ -384,7 +404,7 @@
     rows = image_count * planes * 2
     message = lambda count: pltpu.VMEM((axis_size, count, third_length), jnp.float32)
     row = pltpu.VMEM((1, third_length), jnp.float32)
-    phases = 5 + 3 * image_count
+    phases = 6 + 3 * image_count
     hbm = pl.BlockSpec(memory_space=pltpu.HBM)
     vmem = pl.BlockSpec(memory_space=pltpu.VMEM)
     relaxed, spacing = pl.pallas_call(
@@ -401,7 +421,7 @@
             *[pltpu.VMEM(t.shape, jnp.bfloat16) for t in tables],
             message(2 * rows), message(2 * rows),
             message(rows), message(rows), message(rows), message(rows), message(rows), message(rows),
-            row, row, row, pltpu.VMEM((axis_size // CORES, 1, third_length), jnp.float32),
+            row, row, row, row, row, pltpu.VMEM((axis_size // CORES // CORES, 1, third_length), jnp.float32),
             pltpu.VMEM((image_count, 2, first_length, third_length), jnp.float32),
             pltpu.SemaphoreType.DMA((2 + TABLES,)),
             pltpu.SemaphoreType.DMA((phases,)),

time: 150 us -> 149 us (level)
  no operation moved by 1% of the time
where the time goes in v6:
time: 149 us
  Pallas kernels  147 us (99%)
    pallas_call x1, Pallas kernels, local(): pl.pallas_call(functools.partial(kernel, images.shape, axis_size), out_sh...  147 us

profile of v6, /device:TPU:37, one launch (start us, length us, event | category | flops | bytes accessed | tf_op | source)
XLA Modules:
  0.0 148.8 jit_solution(16446102463971617126)
XLA Ops:
  0.6 146.9 %shard_map.95 = (f32[2,2,128,128]{3,2,1,0:T(8,128)S(1)}, f32[1,2]{1,0:T(1,128)S(1)}) custom-call(f32[2,2,128,128]{3,2,1,0:T(8,128)} %images_hbm.1, f32[2,2]{1,0:T(2,128)} %weights_hbm.1, bf16[2,128,128]{2,1,0:T(8,128)(2,1)} %constant.8.clone.refs_0_.refs_2_, bf16[2,128,128]{2,1,0:T(8,128)(2,1)} %constant.9.clone.refs_1_.refs_3_, ...), custom_call_target="tpu_custom_call" | custom-call | tf_op jit(solution)/shard_map/pallas_call | solution.py:410
  147.6 0.7 copy.12
  148.3 0.5 copy.13
